TPU v7x, 32 devices: a whole 2x2x4 slice. The times are simulated.
32 devices in a mesh: dp: 8 (over z, x), feat: 4 (over y, core).
Axes of the slice: x: 2, y: 2, z: 4, core: 2. Of those that a mesh axis runs over, the one named last changes fastest.
Arguments:
- activations: bfloat16 [2048, 8192], P('dp', 'feat'), may hold values from -6 to 6
- cotangent: bfloat16 [2048, 1024], P('dp'), may hold values from -0.13183594 to 0.13183594
- weight: float32 [8192, 1024], P('feat'), may hold values from -0.0625 to 0.0625
- stats_old: float32 [4, 8, 4, 256, 256], P('feat', 'dp'), as said below
- owners: int32 [32, 4], replicated, may hold values from 0 to 7, as said below
- next_acts: bfloat16 [2048, 8192], P('dp', 'feat'), may hold values from -6 to 6
Outputs:
- weight_new: float32 [8192, 1024], P('feat')
- stats_new: float32 [4, 8, 4, 256, 256], P('feat', 'dp')
- next_out: bfloat16 [2048, 1024], P('dp', 'feat')
Inputs may be any that keep to these rules, and one draw needn't show every extreme that they name: `owners`: blocks are grouped by the index of feat that holds their rows (8192 / (256 * 4) row blocks a group); in every group each dp index owns at most 4 blocks, and some dp index owns exactly 4. `stats_old`: every slot holds a symmetric positive definite matrix; slots that no block maps to are not read.
All inputs are finite; a program needn't handle non-finite values.
Results may differ from a plain program's by a relative error of at most 0.02.
Values may be sent and summed in bfloat16 or wider, within the bound.
A program may use at most 128 MiB of HBM per device.

v0:
```python
import functools

import jax
import jax.numpy as jnp
from jax import lax
from jax.experimental import pallas as pl
from jax.experimental.pallas import tpu as pltpu
from jax.sharding import PartitionSpec as P

ITERS = 6

decay_rate = 0.9
step_rate = 0.01
VMEM_BYTES = 48 * 1024 * 1024
REFRESH_BYTES = 20 * 1024 * 1024
APPLY_BYTES = 16 * 1024 * 1024
TOTAL_BYTES = 4 * 1024 * 1024


def spot(index, count):
    if count % 2:
        return index
    odd = lax.rem(index, 2)
    half = index // 2
    return (1 - odd) * half + odd * (count - 1 - half)


def at_spot(place, count):
    place = lax.rem(place + 2 * count, count)
    if count % 2:
        return place
    far = (2 * place) // count
    return (1 - far) * (2 * place) + far * (2 * (count - place) - 1)


def refresh_kernel(
    n, slots, width, row_ref, col_ref, act_ref, cot_ref, old_hbm, stats_ref, gath_ref,
    act_cut, cot_cut, old_ref, first_ref, acc_ref, grad_ref, mat_ref, iter_ref,
    rs_send, rs_recv, ag_send, ag_recv, act_sem, cot_sem, old_sem,
):
    me = lax.axis_index("dp")
    here = spot(me, n)
    after, before = at_spot(here + 1, n), at_spot(here - 1, n)
    forward = (slots + 1) // 2
    sign = [1 if k < forward else -1 for k in range(slots)]
    turns = sorted(range(slots), key=lambda k: (k % forward, k))
    target = {1: after, -1: before}

    barrier = pltpu.get_barrier_semaphore()
    for peer in (before, after):
        pl.semaphore_signal(
            barrier, inc=1, device_id={"dp": peer}, device_id_type=pl.DeviceIdType.MESH
        )

    cuts = [
        pltpu.make_async_copy(
            cot_ref.at[:, c * width : (c + 1) * width], cot_cut.at[c], cot_sem.at[c]
        )
        for c in range(cot_cut.shape[0])
    ] + [
        pltpu.make_async_copy(
            act_ref.at[:, r * width : (r + 1) * width], act_cut.at[r], act_sem.at[r]
        )
        for r in range(act_cut.shape[0])
    ]
    load_old = pltpu.make_async_copy(old_hbm, old_ref, old_sem)
    for cut in cuts:
        cut.start()
    load_old.start()

    def term(place, k):
        index = at_spot(place, n) * slots + k
        return lax.dot_general(
            act_cut[row_ref[index]],
            cot_cut[col_ref[index]],
            (((0,), (0,)), ((), ())),
            preferred_element_type=jnp.float32,
        )

    def sum_copy(k, step, first=False):
        return pltpu.make_async_remote_copy(
            src_ref=first_ref.at[k] if first else acc_ref.at[k, step - 1],
            dst_ref=acc_ref.at[k, step],
            send_sem=rs_send.at[k, step],
            recv_sem=rs_recv.at[k, step],
            device_id={"dp": target[sign[k]]},
            device_id_type=pl.DeviceIdType.MESH,
        )

    def gather_copy(k, step, owner):
        return pltpu.make_async_remote_copy(
            src_ref=gath_ref.at[owner, k],
            dst_ref=gath_ref.at[owner, k],
            send_sem=ag_send.at[k, step],
            recv_sem=ag_recv.at[k, step],
            device_id={"dp": target[sign[k]]},
            device_id_type=pl.DeviceIdType.MESH,
        )

    for cut in cuts:
        cut.wait()
    for k in turns:
        first_ref[k] = term(here - sign[k], k).astype(jnp.bfloat16)
    pl.semaphore_wait(barrier, 2)
    for k in turns:
        sum_copy(k, 0, True).start()

    def pass_on(step, _):
        for k in turns:
            own = term(here - sign[k] * (2 + step), k)
            sum_copy(k, step, True).wait_recv()
            acc_ref[k, step] = (acc_ref[k, step].astype(jnp.float32) + own).astype(jnp.bfloat16)
            sum_copy(k, step + 1).start()
        return 0

    lax.fori_loop(0, n - 2, pass_on, 0)
    for k in turns:
        own = term(here, k)
        sum_copy(k, n - 2, True).wait_recv()
        grad_ref[k] = (acc_ref[k, n - 2].astype(jnp.float32) + own).astype(jnp.bfloat16)

    load_old.wait()
    row = lax.broadcasted_iota(jnp.int32, (width, width), 0)
    col = lax.broadcasted_iota(jnp.int32, (width, width), 1)
    identity = jnp.where(row == col, 1.0, 0.0).astype(jnp.float32)
    dot = functools.partial(jnp.dot, preferred_element_type=jnp.float32)
    norms = []
    for k in range(slots):
        g = grad_ref[k]
        gram = (
            lax.dot_general(g, g, (((1,), (1,)), ((), ())), preferred_element_type=jnp.float32)
            / width
        )
        renewed = decay_rate * old_ref[k] + (1.0 - decay_rate) * gram
        stats_ref[k] = renewed
        norm = jnp.sqrt(jnp.sum(renewed * renewed, keepdims=True) + 1e-06)
        norms.append(norm)
        mat_ref[k] = renewed / norm

    def factors():
        return [((5.0 * identity - mat_ref[k]) / 4.0).astype(jnp.bfloat16) for k in range(slots)]

    def advance(low):
        square = [dot(low[k], low[k]).astype(jnp.bfloat16) for k in range(slots)]
        fourth = [dot(square[k], square[k]).astype(jnp.bfloat16) for k in range(slots)]
        for k in range(slots):
            mat_ref[k] = dot(fourth[k], mat_ref[k].astype(jnp.bfloat16))

    low = factors()
    for k in range(slots):
        iter_ref[k] = low[k]
    advance(low)

    def newton_step(step, _):
        low = factors()
        for k in range(slots):
            iter_ref[k] = dot(iter_ref[k], low[k]).astype(jnp.bfloat16)
        advance(low)
        return 0

    lax.fori_loop(1, ITERS - 1, newton_step, 0)
    low = factors()
    for k in turns:
        root = dot(iter_ref[k], low[k]) * norms[k] ** (-0.25)
        gath_ref[me, k] = dot(root.astype(jnp.bfloat16), grad_ref[k]).astype(jnp.bfloat16)
        gather_copy(k, 0, me).start()

    def relay(step, _):
        for k in turns:
            owner = at_spot(here - sign[k] * (1 + step), n)
            gather_copy(k, step, owner).wait_recv()
            gather_copy(k, step + 1, owner).start()
        return 0

    lax.fori_loop(0, n - 2, relay, 0)
    for k in turns:
        owner = at_spot(here - sign[k] * (n - 1), n)
        gather_copy(k, n - 2, owner).wait_recv()

    def finish(step, _):
        for k in turns:
            sum_copy(k, step, True).wait_send()
            gather_copy(k, step, me).wait_send()
        return 0

    lax.fori_loop(0, n - 1, finish, 0)


def refresh(n, row_of, col_of, activations, cotangent, old):
    slots, width, _ = old.shape
    tokens = activations.shape[0]
    vmem = pl.BlockSpec(memory_space=pltpu.VMEM)
    smem = pl.BlockSpec(memory_space=pltpu.SMEM)
    hbm = pl.BlockSpec(memory_space=pltpu.HBM)
    dma = pltpu.SemaphoreType.DMA
    low = jnp.bfloat16
    return pl.pallas_call(
        functools.partial(refresh_kernel, n, slots, width),
        out_shape=(
            jax.ShapeDtypeStruct((slots, width, width), jnp.float32),
            jax.ShapeDtypeStruct((n, slots, width, width), low),
        ),
        in_specs=[smem, smem, hbm, hbm, hbm],
        out_specs=(vmem, vmem),
        scratch_shapes=[
            pltpu.VMEM((activations.shape[1] // width, tokens, width), low),
            pltpu.VMEM((cotangent.shape[1] // width, tokens, width), low),
            pltpu.VMEM((slots, width, width), jnp.float32),
            pltpu.VMEM((slots, width, width), low),
            pltpu.VMEM((slots, n - 1, width, width), low),
            pltpu.VMEM((slots, width, width), low),
            pltpu.VMEM((slots, width, width), jnp.float32),
            pltpu.VMEM((slots, width, width), low),
            dma((slots, n - 1)),
            dma((slots, n - 1)),
            dma((slots, n - 1)),
            dma((slots, n - 1)),
            dma((activations.shape[1] // width,)),
            dma((cotangent.shape[1] // width,)),
            dma,
        ],
        compiler_params=pltpu.CompilerParams(
            vmem_limit_bytes=REFRESH_BYTES if n * slots <= 32 else VMEM_BYTES,
            collective_id=0,
            has_side_effects=True,
        ),
        cost_estimate=pl.CostEstimate(
            flops=2 * slots * 31 * width**3, bytes_accessed=100_000_000, transcendentals=0
        ),
        name="refresh",
    )(row_of, col_of, activations, cotangent, old)


def total_kernel(n, part_ref, out_ref, held_ref, send_sem, recv_sem):
    me = lax.axis_index("feat")
    barrier = pltpu.get_barrier_semaphore()
    for d in range(1, n):
        pl.semaphore_signal(
            barrier,
            inc=1,
            device_id={"feat": lax.rem(me + d, n)},
            device_id_type=pl.DeviceIdType.MESH,
        )
    pl.semaphore_wait(barrier, n - 1)
    copies = []
    for d in range(1, n):
        peer = lax.rem(me + d, n)
        copy = pltpu.make_async_remote_copy(
            src_ref=part_ref.at[peer],
            dst_ref=held_ref.at[d - 1],
            send_sem=send_sem.at[d - 1],
            recv_sem=recv_sem.at[d - 1],
            device_id={"feat": peer},
            device_id_type=pl.DeviceIdType.MESH,
        )
        copy.start()
        copies.append(copy)
    total = part_ref[me].astype(jnp.float32)
    for d in range(1, n):
        copies[d - 1].wait_recv()
        total = total + held_ref[d - 1].astype(jnp.float32)
    out_ref[...] = total.astype(out_ref.dtype)
    for copy in copies:
        copy.wait_send()


def total_over_feat(n, parts):
    _, tokens, cols = parts.shape
    vmem = pl.BlockSpec(memory_space=pltpu.VMEM)
    return pl.pallas_call(
        functools.partial(total_kernel, n),
        out_shape=jax.ShapeDtypeStruct((tokens, cols), parts.dtype),
        in_specs=[vmem],
        out_specs=vmem,
        scratch_shapes=[
            pltpu.VMEM((n - 1, tokens, cols), parts.dtype),
            pltpu.SemaphoreType.DMA((n - 1,)),
            pltpu.SemaphoreType.DMA((n - 1,)),
        ],
        compiler_params=pltpu.CompilerParams(
            vmem_limit_bytes=TOTAL_BYTES, collective_id=1, has_side_effects=True
        ),
        name="total_over_feat",
    )(parts)


def apply_kernel(width, col_blocks, splits, place_ref, weight_ref, acts_ref, gath_ref, new_ref, part_ref, acc_ref):
    r = pl.program_id(0)

    @pl.when(r == 0)
    def _():
        acc_ref[...] = jnp.zeros_like(acc_ref)

    for c in range(col_blocks):
        cols = slice(c * width, (c + 1) * width)
        update = gath_ref[place_ref[r * col_blocks + c]]
        fresh = weight_ref[:, cols] - step_rate * update.astype(jnp.float32)
        new_ref[:, cols] = fresh
        acc_ref[:, cols] += jnp.dot(
            acts_ref[...], fresh.astype(jnp.bfloat16), preferred_element_type=jnp.float32
        )

    @pl.when(r == pl.num_programs(0) - 1)
    def _():
        share = acc_ref.shape[1] // splits
        for f in range(splits):
            part_ref[f] = acc_ref[:, f * share : (f + 1) * share].astype(part_ref.dtype)


def apply_update(place, weight, acts, gathered, splits):
    width = gathered.shape[-1]
    rows, cols = weight.shape
    tokens = acts.shape[0]
    share = cols // splits
    return pl.pallas_call(
        functools.partial(apply_kernel, width, cols // width, splits),
        out_shape=(
            jax.ShapeDtypeStruct((rows, cols), jnp.float32),
            jax.ShapeDtypeStruct((splits, tokens, share), jnp.bfloat16),
        ),
        grid_spec=pltpu.PrefetchScalarGridSpec(
            num_scalar_prefetch=1,
            grid=(rows // width,),
            in_specs=[
                pl.BlockSpec((width, cols), lambda i, p: (i, 0)),
                pl.BlockSpec((tokens, width), lambda i, p: (0, i)),
                pl.BlockSpec(
                    gathered.shape, lambda i, p: (0, 0, 0), pipeline_mode=pl.Buffered(1)
                ),
            ],
            out_specs=(
                pl.BlockSpec((width, cols), lambda i, p: (i, 0)),
                pl.BlockSpec((splits, tokens, share), lambda i, p: (0, 0, 0)),
            ),
            scratch_shapes=[pltpu.VMEM((tokens, cols), jnp.float32)],
        ),
        compiler_params=pltpu.CompilerParams(vmem_limit_bytes=APPLY_BYTES if gathered.size <= 1 << 21 else VMEM_BYTES),
        cost_estimate=pl.CostEstimate(
            flops=2 * rows * cols * tokens,
            bytes_accessed=8 * rows * cols + 2 * gathered.size,
            transcendentals=0,
        ),
        name="apply_update",
    )(place, weight, acts, gathered)


def body(n_dp, n_feat, activations, cotangent, weight, stats_old, owners, next_acts):
    width = stats_old.shape[-1]
    slots = stats_old.shape[2]
    rows_dev, columns = weight.shape
    row_blocks = rows_dev // width
    col_blocks = columns // width
    block_count = row_blocks * col_blocks
    feat_index = lax.axis_index("feat")
    data_index = lax.axis_index("dp")
    own_list = lax.dynamic_slice_in_dim(owners, feat_index * row_blocks, row_blocks, 0).reshape(
        block_count
    )
    ids = jnp.arange(block_count, dtype=jnp.int32)
    slot_of = jnp.sum(
        ((own_list[:, None] == own_list[None, :]) & (ids[None, :] < ids[:, None])).astype(jnp.int32),
        axis=1,
    )
    place = own_list * slots + slot_of
    held = place[None, :] == jnp.arange(n_dp * slots, dtype=jnp.int32)[:, None]
    order = jnp.sum(jnp.where(held, ids[None, :], 0), axis=1)
    stats, gathered = refresh(
        n_dp, order // col_blocks, order % col_blocks, activations, cotangent, stats_old[0, 0]
    )
    if n_dp * slots != block_count:
        mine = (own_list == data_index)[None, :] & (slot_of[None, :] == jnp.arange(slots)[:, None])
        stats = jnp.where(jnp.any(mine, axis=1)[:, None, None], stats, 0.0)
    gathered = gathered.reshape(n_dp * slots, width, width)
    direct = columns % (128 * n_feat) == 0
    weight_new, parts = apply_update(
        place, weight, next_acts, gathered, n_feat if direct else 1
    )
    if direct:
        next_out = total_over_feat(n_feat, parts)
    else:
        next_out = lax.psum_scatter(parts[0], "feat", scatter_dimension=1, tiled=True)
    return (weight_new, stats[None, None], next_out)


def solution(mesh):
    placed = (
        P("dp", "feat"),
        P("dp", None),
        P("feat", None),
        P("feat", "dp", None, None, None),
        P(),
        P("dp", "feat"),
    )
    return jax.shard_map(
        functools.partial(body, mesh.shape["dp"], mesh.shape["feat"]),
        mesh=mesh,
        in_specs=placed,
        out_specs=(P("feat", None), P("feat", "dp", None, None, None), P("dp", "feat")),
        check_vma=False,
    )
```

profile of v0, /device:TPU:1, one launch (start us, length us, event | category | flops | bytes accessed | tf_op | source)
XLA Modules:
  0.0 114.3 jit_solution(4309737403246512769)
XLA Ops:
  0.6 0.0 copy-start
  0.6 0.0 copy-start.1
  0.7 0.7 copy-done
  1.3 0.1 constant_dynamic-slice_fusion
  1.4 0.1 copy.11
  1.5 0.1 reshape.22
  1.6 0.0 slice-start
  1.6 0.2 convert_reduce_fusion
  1.7 0.1 select_reduce_fusion
  1.9 0.0 copy-start.2
  1.9 1.4 %copy-done.2 = bf16[256,2048]{1,0:T(8,128)(2,1)S(1)} copy-done((bf16[256,2048]{1,0:T(8,128)(2,1)S(1)}, bf16[256,2048]{1,0:T(8,128)(2,1)}, u32[]{:S(2)}) %copy-start.2) | copy-done | bytes 1048600
  3.3 0.0 copy-start.3
  3.3 1.2 %copy-done.3 = f32[1,1,4,256,256]{4,3,2,1,0:T(8,128)S(1)} copy-done((f32[1,1,4,256,256]{4,3,2,1,0:T(8,128)S(1)}, f32[1,1,4,256,256]{4,3,2,1,0:T(8,128)}, u32[]{:S(2)}) %copy-start.3) | copy-done | bytes 1048600
  4.5 0.0 copy-start.4
  4.5 1.0 copy-done.4
  5.5 0.0 slice-start.1
  5.5 89.2 %refresh.1 = (f32[4,256,256]{2,1,0:T(8,128)S(1)}, bf16[8,4,256,256]{3,2,1,0:T(8,128)(2,1)S(1)}) custom-call(s32[32]{0:T(128)S(1)} %get-tuple-element.12.row_ref, s32[32]{0:T(128)S(1)} %get-tuple-element.11.col_ref, bf16[256,2048]{1,0:T(8,128)(2,1)S(1)} %copy-done.2, bf16[256,1024]{1,0:T(8,128)(2,1)S(1)} %copy-done.4, f32[4,256,256]{2,1,0:T(8,128)S(1)} %bitcast.7), custom_call_target="tpu_custom_call" | custom-call | flops 4160749568 | bytes 100000000 | tf_op jit(solution)/shard_map/refresh/pallas_call | solution.py:197
  94.8 0.0 copy-done.1
  94.8 0.0 slice-done
  94.8 0.0 slice-done.1
  94.8 6.5 %apply_update.1 = (f32[2048,1024]{1,0:T(8,128)}, bf16[4,256,256]{2,1,0:T(8,128)(2,1)S(1)}) custom-call(s32[32]{0:T(128)S(1)} %multiply_add_fusion.place_ref, f32[2048,1024]{1,0:T(8,128)S(1)} %bitcast.4, bf16[256,2048]{1,0:T(8,128)(2,1)S(1)} %copy-done.1, bf16[32,256,256]{2,1,0:T(8,128)(2,1)S(1)} %bitcast.5), custom_call_target="tpu_custom_call" | custom-call | flops 1073741824 | bytes 20971520 | tf_op jit(solution)/shard_map/apply_update/pallas_call | solution.py:315
  101.3 11.4 %total_over_feat.1 = bf16[256,256]{1,0:T(8,128)(2,1)S(1)} custom-call(bf16[4,256,256]{2,1,0:T(8,128)(2,1)S(1)} %get-tuple-element.10.part_ref), custom_call_target="tpu_custom_call" | custom-call | tf_op jit(solution)/shard_map/total_over_feat/pallas_call | solution.py:270
  112.7 1.0 copy.14
  113.7 0.7 copy.15
  (3 shorter events, 0.0 us)
Async XLA Ops:
  0.6 0.7 copy-start
  0.6 94.2 %copy-start.1 = (bf16[256,2048]{1,0:T(8,128)(2,1)S(1)}, bf16[256,2048]{1,0:T(8,128)(2,1)}, u32[]{:S(2)}) copy-start(bf16[256,2048]{1,0:T(8,128)(2,1)} %acts_ref.1) | copy-start | bytes 3145732
  1.6 93.3 %slice-start = ((s8[8388608]{0:T(1024)(128)(4,1)}), s8[4194304]{0:T(1024)(128)(4,1)S(1)}, s32[]{:S(2)}) async-start(s8[8388608]{0:T(1024)(128)(4,1)} %bitcast.3), calls=%async_computation | async-start | bytes 8388608
  1.9 1.4 %copy-start.2 = (bf16[256,2048]{1,0:T(8,128)(2,1)S(1)}, bf16[256,2048]{1,0:T(8,128)(2,1)}, u32[]{:S(2)}) copy-start(bf16[256,2048]{1,0:T(8,128)(2,1)} %act_ref.1) | copy-start | bytes 3145732
  3.3 1.2 %copy-start.3 = (f32[1,1,4,256,256]{4,3,2,1,0:T(8,128)S(1)}, f32[1,1,4,256,256]{4,3,2,1,0:T(8,128)}, u32[]{:S(2)}) copy-start(f32[1,1,4,256,256]{4,3,2,1,0:T(8,128)} %param.9) | copy-start | bytes 3145732
  4.5 1.0 copy-start.4
  5.5 89.3 %slice-start.1 = ((s8[8388608]{0:T(1024)(128)(4,1)}), s8[4194304]{0:T(1024)(128)(4,1)S(1)}, s32[]{:S(2)}) async-start(s8[8388608]{0:T(1024)(128)(4,1)} %bitcast.3), calls=%async_computation.1 | async-start | bytes 8388608
where the time goes:
time: 115 us; the launch traced here: 114 us
  Pallas kernels  107 us (93%)
  local copies, waits for them, and re-layouts  6.18 us (5%)
    pallas_call x1, Pallas kernels, refresh(): pl.pallas_call(functools.partial(refresh_kernel, n, slots, width), out_sh...  89.2 us
    pallas_call x1, Pallas kernels, total_over_feat(): pl.pallas_call(functools.partial(total_kernel, n), out_shape=jax.ShapeDty...  11.4 us
    pallas_call x1, Pallas kernels, apply_update(): pl.pallas_call(functools.partial(apply_kernel, width, cols // width, spli...  6.48 us
    unnamed x16, local copies, waits for them, and re-layouts  5.94 us

commit v1 on v0

--- a/solution.py
+++ b/solution.py
@@ -13,7 +13,7 @@
 step_rate = 0.01
 VMEM_BYTES = 48 * 1024 * 1024
 REFRESH_BYTES = 20 * 1024 * 1024
-APPLY_BYTES = 16 * 1024 * 1024
+APPLY_BYTES = 36 * 1024 * 1024
 TOTAL_BYTES = 4 * 1024 * 1024
 
 
@@ -228,54 +228,86 @@
             flops=2 * slots * 31 * width**3, bytes_accessed=100_000_000, transcendentals=0
         ),
         name="refresh",
-    )(row_of, col_of, activations, cotangent, old)
-
-
-def total_kernel(n, part_ref, out_ref, held_ref, send_sem, recv_sem):
+    )(row_of, col_of, *(pltpu.with_memory_space_constraint(x, pltpu.HBM) for x in (activations, cotangent, old)))
+
+
+def total_kernel(n, part_ref, out_ref, near_ref, pair_ref, far_ref, near_send, near_recv, far_send, far_recv):
     me = lax.axis_index("feat")
+    core = lax.rem(me, 2)
+    here = me // 2
+    chips = n // 2
+    partner = here * 2 + 1 - core
     barrier = pltpu.get_barrier_semaphore()
-    for d in range(1, n):
+    peers = [lax.rem(here + d, chips) * 2 + core for d in range(1, chips)]
+    for peer in peers + [partner]:
         pl.semaphore_signal(
-            barrier,
-            inc=1,
-            device_id={"feat": lax.rem(me + d, n)},
+            barrier, inc=1, device_id={"feat": peer}, device_id_type=pl.DeviceIdType.MESH
+        )
+    pl.semaphore_wait(barrier, chips)
+
+    def near_copy(d):
+        place = lax.rem(here + d, chips) * 2 + 1 - core
+        return pltpu.make_async_remote_copy(
+            src_ref=part_ref.at[place],
+            dst_ref=near_ref.at[d],
+            send_sem=near_send.at[d],
+            recv_sem=near_recv.at[d],
+            device_id={"feat": partner},
             device_id_type=pl.DeviceIdType.MESH,
         )
-    pl.semaphore_wait(barrier, n - 1)
-    copies = []
-    for d in range(1, n):
-        peer = lax.rem(me + d, n)
-        copy = pltpu.make_async_remote_copy(
-            src_ref=part_ref.at[peer],
-            dst_ref=held_ref.at[d - 1],
-            send_sem=send_sem.at[d - 1],
-            recv_sem=recv_sem.at[d - 1],
-            device_id={"feat": peer},
+
+    def far_copy(d):
+        return pltpu.make_async_remote_copy(
+            src_ref=pair_ref.at[d - 1],
+            dst_ref=far_ref.at[d - 1],
+            send_sem=far_send.at[d - 1],
+            recv_sem=far_recv.at[d - 1],
+            device_id={"feat": peers[d - 1]},
             device_id_type=pl.DeviceIdType.MESH,
         )
-        copy.start()
-        copies.append(copy)
-    total = part_ref[me].astype(jnp.float32)
-    for d in range(1, n):
-        copies[d - 1].wait_recv()
-        total = total + held_ref[d - 1].astype(jnp.float32)
+
+    def pair_sum(d):
+        place = lax.rem(here + d, chips) * 2 + core
+        own = part_ref[place].astype(jnp.float32)
+        return own + near_ref[d].astype(jnp.float32)
+
+    turns = list(range(1, chips)) + [0]
+    for d in turns:
+        near_copy(d).start()
+    for d in turns[:-1]:
+        near_copy(d).wait_recv()
+        pair_ref[d - 1] = pair_sum(d).astype(pair_ref.dtype)
+        far_copy(d).start()
+    near_copy(0).wait_recv()
+    total = pair_sum(0)
+    for d in turns[:-1]:
+        far_copy(d).wait_recv()
+        total = total + far_ref[d - 1].astype(jnp.float32)
     out_ref[...] = total.astype(out_ref.dtype)
-    for copy in copies:
-        copy.wait_send()
+    for d in turns:
+        near_copy(d).wait_send()
+    for d in turns[:-1]:
+        far_copy(d).wait_send()
 
 
 def total_over_feat(n, parts):
     _, tokens, cols = parts.shape
     vmem = pl.BlockSpec(memory_space=pltpu.VMEM)
+    dma = pltpu.SemaphoreType.DMA
+    chips = n // 2
     return pl.pallas_call(
         functools.partial(total_kernel, n),
         out_shape=jax.ShapeDtypeStruct((tokens, cols), parts.dtype),
         in_specs=[vmem],
         out_specs=vmem,
         scratch_shapes=[
-            pltpu.VMEM((n - 1, tokens, cols), parts.dtype),
-            pltpu.SemaphoreType.DMA((n - 1,)),
-            pltpu.SemaphoreType.DMA((n - 1,)),
+            pltpu.VMEM((chips, tokens, cols), parts.dtype),
+            pltpu.VMEM((chips - 1, tokens, cols), parts.dtype),
+            pltpu.VMEM((chips - 1, tokens, cols), parts.dtype),
+            dma((chips,)),
+            dma((chips,)),
+            dma((chips - 1,)),
+            dma((chips - 1,)),
         ],
         compiler_params=pltpu.CompilerParams(
             vmem_limit_bytes=TOTAL_BYTES, collective_id=1, has_side_effects=True
@@ -284,56 +316,63 @@
     )(parts)
 
 
-def apply_kernel(width, col_blocks, splits, place_ref, weight_ref, acts_ref, gath_ref, new_ref, part_ref, acc_ref):
-    r = pl.program_id(0)
-
-    @pl.when(r == 0)
-    def _():
-        acc_ref[...] = jnp.zeros_like(acc_ref)
-
+def apply_kernel(
+    width, col_blocks, splits, place_ref, weight_ref, acts_ref, gath_ref, stats_ref,
+    new_hbm, part_ref, stats_hbm, fresh_ref, low_ref, new_sem, stats_sem,
+):
+    row_blocks = weight_ref.shape[0] // width
+    share = weight_ref.shape[1] // splits
+    keep = pltpu.make_async_copy(stats_ref, stats_hbm, stats_sem)
+    keep.start()
+    writes = []
     for c in range(col_blocks):
         cols = slice(c * width, (c + 1) * width)
-        update = gath_ref[place_ref[r * col_blocks + c]]
-        fresh = weight_ref[:, cols] - step_rate * update.astype(jnp.float32)
-        new_ref[:, cols] = fresh
-        acc_ref[:, cols] += jnp.dot(
-            acts_ref[...], fresh.astype(jnp.bfloat16), preferred_element_type=jnp.float32
-        )
-
-    @pl.when(r == pl.num_programs(0) - 1)
-    def _():
-        share = acc_ref.shape[1] // splits
-        for f in range(splits):
-            part_ref[f] = acc_ref[:, f * share : (f + 1) * share].astype(part_ref.dtype)
-
-
-def apply_update(place, weight, acts, gathered, splits):
+        for r in range(row_blocks):
+            rows = slice(r * width, (r + 1) * width)
+            update = gath_ref[place_ref[r * col_blocks + c]]
+            fresh = weight_ref[rows, cols] - step_rate * update.astype(jnp.float32)
+            fresh_ref[rows, cols] = fresh
+            low_ref[c, rows, :] = fresh.astype(jnp.bfloat16)
+        write = pltpu.make_async_copy(
+            fresh_ref.at[:, cols], new_hbm.at[:, cols], new_sem.at[c]
+        )
+        write.start()
+        writes.append(write)
+        part = jnp.dot(acts_ref[...], low_ref[c], preferred_element_type=jnp.float32)
+        part = part.astype(part_ref.dtype)
+        if share >= width:
+            spot_in = (c * width) % share
+            part_ref[(c * width) // share, :, spot_in : spot_in + width] = part
+        else:
+            for f in range(width // share):
+                part_ref[(c * width) // share + f] = part[:, f * share : (f + 1) * share]
+    for write in writes:
+        write.wait()
+    keep.wait()
+
+
+def apply_update(place, weight, acts, gathered, stats, splits):
     width = gathered.shape[-1]
     rows, cols = weight.shape
     tokens = acts.shape[0]
     share = cols // splits
+    vmem = pl.BlockSpec(memory_space=pltpu.VMEM)
+    hbm = pl.BlockSpec(memory_space=pltpu.HBM)
     return pl.pallas_call(
         functools.partial(apply_kernel, width, cols // width, splits),
         out_shape=(
             jax.ShapeDtypeStruct((rows, cols), jnp.float32),
             jax.ShapeDtypeStruct((splits, tokens, share), jnp.bfloat16),
-        ),
-        grid_spec=pltpu.PrefetchScalarGridSpec(
-            num_scalar_prefetch=1,
-            grid=(rows // width,),
-            in_specs=[
-                pl.BlockSpec((width, cols), lambda i, p: (i, 0)),
-                pl.BlockSpec((tokens, width), lambda i, p: (0, i)),
-                pl.BlockSpec(
-                    gathered.shape, lambda i, p: (0, 0, 0), pipeline_mode=pl.Buffered(1)
-                ),
-            ],
-            out_specs=(
-                pl.BlockSpec((width, cols), lambda i, p: (i, 0)),
-                pl.BlockSpec((splits, tokens, share), lambda i, p: (0, 0, 0)),
-            ),
-            scratch_shapes=[pltpu.VMEM((tokens, cols), jnp.float32)],
-        ),
+            jax.ShapeDtypeStruct(stats.shape, stats.dtype),
+        ),
+        in_specs=[pl.BlockSpec(memory_space=pltpu.SMEM), vmem, vmem, vmem, vmem],
+        out_specs=(hbm, vmem, hbm),
+        scratch_shapes=[
+            pltpu.VMEM((rows, cols), jnp.float32),
+            pltpu.VMEM((cols // width, rows, width), jnp.bfloat16),
+            pltpu.SemaphoreType.DMA((cols // width,)),
+            pltpu.SemaphoreType.DMA,
+        ],
         compiler_params=pltpu.CompilerParams(vmem_limit_bytes=APPLY_BYTES if gathered.size <= 1 << 21 else VMEM_BYTES),
         cost_estimate=pl.CostEstimate(
             flops=2 * rows * cols * tokens,
@@ -341,7 +380,7 @@
             transcendentals=0,
         ),
         name="apply_update",
-    )(place, weight, acts, gathered)
+    )(place, weight, acts, gathered, stats)
 
 
 def body(n_dp, n_feat, activations, cotangent, weight, stats_old, owners, next_acts):
@@ -371,9 +410,9 @@
         mine = (own_list == data_index)[None, :] & (slot_of[None, :] == jnp.arange(slots)[:, None])
         stats = jnp.where(jnp.any(mine, axis=1)[:, None, None], stats, 0.0)
     gathered = gathered.reshape(n_dp * slots, width, width)
-    direct = columns % (128 * n_feat) == 0
-    weight_new, parts = apply_update(
-        place, weight, next_acts, gathered, n_feat if direct else 1
+    direct = columns % (128 * n_feat) == 0 and n_feat % 2 == 0 and n_feat > 2
+    weight_new, parts, stats = apply_update(
+        place, weight, next_acts, gathered, stats, n_feat if direct else 1
     )
     if direct:
         next_out = total_over_feat(n_feat, parts)

time: 115 us -> 109 us (0.948)
  local copies, waits for them, and re-layouts: 6.18 us -> 1.58 us
  Pallas kernels: 107 us -> 105 us
    unnamed x16 -> x9, local copies, waits for them, and re-layouts: 5.94 us -> 1.34 us
    pallas_call x1, Pallas kernels: 11.4 us -> 9.81 us  [total_over_feat(): pl.pallas_call(functools.partial(total_kernel, n), out_shape=jax.ShapeDty...]
    pallas_call x1, Pallas kernels: 6.48 us -> 5.22 us  [apply_update(): pl.pallas_call(functools.partial(apply_kernel, width, cols // width, spli...]
where the time goes in v1:
time: 109 us; the launch traced here: 108 us
  Pallas kernels  105 us (96%)
  local copies, waits for them, and re-layouts  1.58 us (1%)
    pallas_call x1, Pallas kernels, refresh(): pl.pallas_call(functools.partial(refresh_kernel, n, slots, width), out_sh...  90.4 us
    pallas_call x1, Pallas kernels, total_over_feat(): pl.pallas_call(functools.partial(total_kernel, n), out_shape=jax.ShapeDty...  9.81 us
    pallas_call x1, Pallas kernels, apply_update(): pl.pallas_call(functools.partial(apply_kernel, width, cols // width, spli...  5.22 us

profile of v1, /device:TPU:1, one launch (start us, length us, event | category | flops | bytes accessed | tf_op | source)
XLA Modules:
  0.0 108.0 jit_solution(12840927499329817923)
XLA Ops:
  0.6 0.0 copy-start
  0.6 0.0 copy-start.1
  0.7 0.7 copy-done
  1.3 0.1 constant_dynamic-slice_fusion
  1.4 0.1 copy.11
  1.5 0.1 reshape.22
  1.6 0.0 slice-start
  1.6 0.2 convert_reduce_fusion
  1.7 0.1 select_reduce_fusion
  1.9 0.0 slice-start.1
  1.9 90.4 %refresh.1 = (f32[4,256,256]{2,1,0:T(8,128)S(1)}, bf16[8,4,256,256]{3,2,1,0:T(8,128)(2,1)S(1)}) custom-call(s32[32]{0:T(128)S(1)} %get-tuple-element.14.row_ref, s32[32]{0:T(128)S(1)} %get-tuple-element.13.col_ref, bf16[256,2048]{1,0:T(8,128)(2,1)} %act_ref.1, bf16[256,1024]{1,0:T(8,128)(2,1)} %cot_ref.1, f32[4,256,256]{2,1,0:T(8,128)} %bitcast.6), custom_call_target="tpu_custom_call" | custom-call | flops 4160749568 | bytes 100000000 | tf_op jit(solution)/shard_map/refresh/pallas_call | solution.py:197
  92.3 0.0 copy-done.1
  92.3 0.0 slice-done
  92.3 0.0 slice-done.1
  92.3 5.2 %apply_update.1 = (f32[2048,1024]{1,0:T(8,128)}, bf16[4,256,256]{2,1,0:T(8,128)(2,1)S(1)}, f32[4,256,256]{2,1,0:T(8,128)}) custom-call(s32[32]{0:T(128)S(1)} %multiply_add_fusion.place_ref, f32[2048,1024]{1,0:T(8,128)S(1)} %bitcast.4, bf16[256,2048]{1,0:T(8,128)(2,1)S(1)} %copy-done.1, bf16[32,256,256]{2,1,0:T(8,128)(2,1)S(1)} %bitcast.5, ...), custom_call_target="tpu_custom_call" | custom-call | flops 1073741824 | bytes 20971520 | tf_op jit(solution)/shard_map/apply_update/pallas_call | solution.py:361
  97.5 9.8 %total_over_feat.1 = bf16[256,256]{1,0:T(8,128)(2,1)S(1)} custom-call(bf16[4,256,256]{2,1,0:T(8,128)(2,1)S(1)} %get-tuple-element.12.part_ref), custom_call_target="tpu_custom_call" | custom-call | tf_op jit(solution)/shard_map/total_over_feat/pallas_call | solution.py:298
  107.4 0.7 copy.13
  (3 shorter events, 0.0 us)
Async XLA Ops:
  0.6 0.7 copy-start
  0.6 91.6 %copy-start.1 = (bf16[256,2048]{1,0:T(8,128)(2,1)S(1)}, bf16[256,2048]{1,0:T(8,128)(2,1)}, u32[]{:S(2)}) copy-start(bf16[256,2048]{1,0:T(8,128)(2,1)} %acts_ref.1) | copy-start | bytes 3145732
  1.6 90.7 %slice-start = ((s8[8388608]{0:T(1024)(128)(4,1)}), s8[4194304]{0:T(1024)(128)(4,1)S(1)}, s32[]{:S(2)}) async-start(s8[8388608]{0:T(1024)(128)(4,1)} %bitcast.3), calls=%async_computation | async-start | bytes 8388608
  1.9 90.4 %slice-start.1 = ((s8[8388608]{0:T(1024)(128)(4,1)}), s8[4194304]{0:T(1024)(128)(4,1)S(1)}, s32[]{:S(2)}) async-start(s8[8388608]{0:T(1024)(128)(4,1)} %bitcast.3), calls=%async_computation.1 | async-start | bytes 8388608
